TPU v7x, 32 devices: a whole 2x2x4 slice. The times are simulated.
32 devices in a mesh: sub: 8 (over z, core), sta: 4 (over y, x).
Axes of the slice: x: 2, y: 2, z: 4, core: 2. Of those that a mesh axis runs over, the one named last changes fastest.
Arguments:
- voltages: bfloat16 [8, 2, 64, 65536], P('sub', None, 'sta'), may hold values from -6 to 6
- beam_weights: bfloat16 [8, 2, 32, 64], P('sub'), may hold values from -0.5 to 0.5
- station_delays: int32 [64], P('sta'), may hold values from 0 to 16383
- dm_index: int32 [32, 1], P('sta'), may hold values from 1 to 8
Outputs:
- dedispersed: float32 [8, 2, 32, 1, 65536], P(None, None, None, None, ('sub', 'sta'))
- intensity: float32 [32, 1, 65536], P(None, None, ('sub', 'sta'))
Inputs may be any that keep to these rules, and one draw needn't show every extreme that they name: `station_delays`: delays in whole samples. `dm_index`: dispersion measure in steps of 10.
All inputs are finite; a program needn't handle non-finite values.
Results may differ from a plain program's by a relative error of at most 0.0006.
Values may be sent and summed in bfloat16 or wider, within the bound.
A program may use at most 320 MiB of HBM per device.

v0:
```python
import jax
import jax.numpy as jnp
from jax import lax
from jax.sharding import PartitionSpec as P

ROOT = 256
TWO_PI = 6.283185307179586
DISPERSION = 4148808000.0
DM_STEP = 10.0
BASE_FREQ = 120.0
CHANNEL_WIDTH = 0.1953125
HIGHEST = lax.Precision.HIGHEST


def angle_tables(rows_len, modulus):
    first = jnp.arange(rows_len, dtype=jnp.int32)[:, None]
    second = jnp.arange(rows_len, dtype=jnp.int32)[None, :]
    product = first * second % modulus
    angles = TWO_PI * product.astype(jnp.float32) / modulus
    return (jnp.cos(angles), jnp.sin(angles))


def chirp_base(subband, root_len, total_len):
    first = jnp.arange(root_len, dtype=jnp.int32)[:, None]
    second = jnp.arange(root_len, dtype=jnp.int32)[None, :]
    positions = first + root_len * second
    signed_bin = jnp.where(positions < total_len // 2, positions, positions - total_len)
    offset = (CHANNEL_WIDTH * signed_bin.astype(jnp.float32) / total_len)[None]
    centre = (BASE_FREQ + CHANNEL_WIDTH * (subband.astype(jnp.float32) + 0.5))[:, None, None]
    return TWO_PI * DISPERSION * offset * offset / (centre * centre * (centre + offset))


def left_dft(cos_table, sin_table, x_real, x_imag, flip_sign):
    real_part = jnp.einsum(
        "kt,...tu->...ku", cos_table, x_real, precision=HIGHEST
    ) + flip_sign * jnp.einsum("kt,...tu->...ku", sin_table, x_imag, precision=HIGHEST)
    imag_part = jnp.einsum(
        "kt,...tu->...ku", cos_table, x_imag, precision=HIGHEST
    ) - flip_sign * jnp.einsum("kt,...tu->...ku", sin_table, x_real, precision=HIGHEST)
    return (real_part, imag_part)


def right_dft(cos_table, sin_table, x_real, x_imag, flip_sign):
    real_part = jnp.einsum(
        "...kt,tm->...km", x_real, cos_table, precision=HIGHEST
    ) + flip_sign * jnp.einsum("...kt,tm->...km", x_imag, sin_table, precision=HIGHEST)
    imag_part = jnp.einsum(
        "...kt,tm->...km", x_imag, cos_table, precision=HIGHEST
    ) - flip_sign * jnp.einsum("...kt,tm->...km", x_real, sin_table, precision=HIGHEST)
    return (real_part, imag_part)


def beam_terms(w_block, v_real, v_imag):
    w_real = w_block[:, 0]
    w_imag = w_block[:, 1]
    real_part = jnp.einsum(
        "sbk,skt->bst", w_real, v_real, preferred_element_type=jnp.float32
    ) - jnp.einsum("sbk,skt->bst", w_imag, v_imag, preferred_element_type=jnp.float32)
    imag_part = jnp.einsum(
        "sbk,skt->bst", w_real, v_imag, preferred_element_type=jnp.float32
    ) + jnp.einsum("sbk,skt->bst", w_imag, v_real, preferred_element_type=jnp.float32)
    return jnp.stack([real_part, imag_part], axis=2)


def shards(voltages, beam_weights, station_delays, dm_index):
    sub_dev = voltages.shape[0]
    total_len = voltages.shape[3]
    local_beams = dm_index.shape[0]
    trials = dm_index.shape[1]
    root_len = ROOT
    doubled = jnp.concatenate([voltages, voltages], axis=3)
    shifted = jax.vmap(
        lambda rows, shift_by: lax.dynamic_slice_in_dim(rows, total_len - shift_by, total_len, 2),
        in_axes=(2, 0),
        out_axes=2,
    )(doubled, station_delays)
    own_weights = lax.dynamic_slice_in_dim(
        beam_weights, lax.axis_index("sta") * local_beams, local_beams, 2
    )
    shard_piece = lax.all_gather(shifted, "sta", axis=2, tiled=True)
    beams = beam_terms(own_weights, shard_piece[:, 0], shard_piece[:, 1])
    cos_root, sin_root = angle_tables(root_len, root_len)
    cos_twist, sin_twist = angle_tables(root_len, total_len)
    x_real = beams[:, :, 0].reshape(local_beams, sub_dev, root_len, root_len)
    x_imag = beams[:, :, 1].reshape(local_beams, sub_dev, root_len, root_len)
    a_real, a_imag = left_dft(cos_root, sin_root, x_real, x_imag, 1.0)
    b_real = a_real * cos_twist + a_imag * sin_twist
    b_imag = a_imag * cos_twist - a_real * sin_twist
    s_real, s_imag = right_dft(cos_root, sin_root, b_real, b_imag, 1.0)
    subband = lax.axis_index("sub") * sub_dev + jnp.arange(sub_dev, dtype=jnp.int32)
    base_phase = chirp_base(subband, root_len, total_len)
    dm_value = DM_STEP * dm_index.astype(jnp.float32)
    phase_table = dm_value[:, None, :, None, None] * base_phase[None, :, None, :, :]
    h_real = jnp.cos(phase_table)
    h_imag = jnp.sin(phase_table)
    c_real = s_real[:, :, None] * h_real - s_imag[:, :, None] * h_imag
    c_imag = s_real[:, :, None] * h_imag + s_imag[:, :, None] * h_real
    d_real, d_imag = right_dft(cos_root, sin_root, c_real, c_imag, -1.0)
    e_real = d_real * cos_twist - d_imag * sin_twist
    e_imag = d_imag * cos_twist + d_real * sin_twist
    scale = 1.0 / total_len
    out_real = jnp.einsum("tk,bsjku->sbjtu", cos_root, e_real, precision=HIGHEST) - jnp.einsum(
        "tk,bsjku->sbjtu", sin_root, e_imag, precision=HIGHEST
    )
    out_imag = jnp.einsum("tk,bsjku->sbjtu", cos_root, e_imag, precision=HIGHEST) + jnp.einsum(
        "tk,bsjku->sbjtu", sin_root, e_real, precision=HIGHEST
    )
    series = jnp.stack([out_real * scale, out_imag * scale], axis=1).reshape(
        sub_dev, 2, local_beams, trials, total_len
    )
    n_sub = lax.axis_size("sub")
    n_sta = lax.axis_size("sta")
    moved = lax.all_to_all(series[None], ("sub", "sta"), split_axis=5, concat_axis=0, tiled=True)
    moved = moved.reshape(n_sub, n_sta, sub_dev, 2, local_beams, trials, -1)
    moved = moved.transpose(0, 2, 3, 1, 4, 5, 6).reshape(
        n_sub * sub_dev, 2, n_sta * local_beams, trials, -1
    )
    intensity = jnp.mean(moved[:, 0] * moved[:, 0] + moved[:, 1] * moved[:, 1], axis=0)
    return (moved, intensity)


def solution(mesh):
    return jax.shard_map(
        shards,
        mesh=mesh,
        in_specs=(
            P("sub", None, "sta", None),
            P("sub", None, None, None),
            P("sta"),
            P("sta", None),
        ),
        out_specs=(P(None, None, None, None, ("sub", "sta")), P(None, None, ("sub", "sta"))),
        check_vma=False,
    )
```

profile of v0, /device:TPU:0, one launch (start us, length us, event | category | flops | bytes accessed | tf_op | source)
XLA Modules:
  0.0 1215.7 jit_solution(15129982250046369785)
XLA Ops:
  7.2 0.7 fusion.83
  7.9 6.5 copy.86
  14.4 9.1 maximum_bitcast_fusion
  23.6 62.1 %while.1 = (s32[]{:T(128)}, bf16[16,1,2,131072]{3,2,1,0:T(2,128)(2,1)}, s32[16,4]{0,1:T(4,128)S(1)}, bf16[16,1,2,65536]{3,2,1,0:T(2,128)(2,1)}, s32[]{:T(128)}) while((s32[]{:T(128)}, bf16[16,1,2,131072]{3,2,1,0:T(2,128)(2,1)}, s32[16,4]{0,1:T(4,128)S(1)}, bf16[16,1,2,65536]{3,2,1,0:T(2,128)(2,1)}, s32[]{:T(128)}) %tuple.27), condition=%wide.while_cond, body=%wide.while_body.sunk | while | flops 2 | bytes 525437 | solution.py:73
  23.6 0.6 fusion.162
  24.2 3.2 dynamic-slice_dynamic-update-slice_fusion.2
  27.5 0.6 fusion.162
  28.1 3.2 dynamic-slice_dynamic-update-slice_fusion.2
  31.4 0.6 fusion.162
  32.0 3.2 dynamic-slice_dynamic-update-slice_fusion.2
  35.3 0.6 fusion.162
  35.9 3.2 dynamic-slice_dynamic-update-slice_fusion.2
  39.7 3.2 dynamic-slice_dynamic-update-slice_fusion.2
  43.6 3.2 dynamic-slice_dynamic-update-slice_fusion.2
  47.5 3.2 dynamic-slice_dynamic-update-slice_fusion.2
  51.4 3.2 dynamic-slice_dynamic-update-slice_fusion.2
  55.3 3.2 dynamic-slice_dynamic-update-slice_fusion.2
  59.2 3.2 dynamic-slice_dynamic-update-slice_fusion.2
  63.0 3.2 dynamic-slice_dynamic-update-slice_fusion.2
  66.9 3.2 dynamic-slice_dynamic-update-slice_fusion.2
  70.8 3.2 dynamic-slice_dynamic-update-slice_fusion.2
  74.7 3.2 dynamic-slice_dynamic-update-slice_fusion.2
  78.6 3.2 dynamic-slice_dynamic-update-slice_fusion.2
  82.4 3.2 dynamic-slice_dynamic-update-slice_fusion.2
  85.7 6.4 copy.122
  92.1 1.0 fusion.63
  93.6 158.7 %all-gather.2.cloned.1.call-done = bf16[1,2,64,65536]{3,2,1,0:T(8,128)(2,1)} async-done(((bf16[1,2,16,65536]{3,2,1,0:T(8,128)(2,1)}), bf16[1,2,64,65536]{3,2,1,0:T(8,128)(2,1)}) %all-gather.2.cloned.1.call-update) | async-done | bytes 16777232 | tf_op jit(solution)/shard_map/all_gather | solution.py:80
  252.3 4.6 fusion.1
  256.9 6.1 convolution_add_fusion
  263.0 2.5 copy.90
  265.4 4.1 fusion.50
  269.5 4.6 fusion
  274.1 6.1 convolution_subtract_fusion
  280.2 3.0 copy.89
  283.3 4.6 fusion.52
  287.8 2.9 convolution_subtract_fusion.1
  290.8 2.9 convolution_add_fusion.1
  293.7 4.9 fusion.25
  298.5 4.6 fusion.27
  303.1 4.6 fusion.20
  307.7 5.1 fusion.17
  312.8 10.3 fusion.44
  323.1 10.2 fusion.46
  333.3 10.4 multiply_subtract_fusion.1
  343.7 10.6 multiply_add_fusion.1
  354.4 4.7 fusion.24
  359.1 5.7 fusion.23
  364.8 5.8 multiply_bitcast_fusion
  370.7 3.1 copy.104
  373.8 3.3 stack.10
  377.1 7.9 multiply_bitcast_fusion.1
  385.0 1.9 copy.101
  386.9 1.7 stack.9
  388.6 4.5 pad_maximum_fusion
  393.1 114.7 %copy.105 = f32[1,1,2,8,1,65536]{3,4,2,1,0,5:T(1,128)} copy(f32[1,1,2,8,1,65536]{5,3,4,2,1,0:T(8,128)} %pad_maximum_fusion) | data formatting | bytes 8388608 | tf_op jit(solution)/shard_map/stack | solution.py:108
  508.3 240.9 %reduce.2 = f32[65536,2,8]{2,1,0:T(2,128)} reduce(f32[65536,1,1,2,1,8]{5,4,3,2,1,0:T(1,128)} %bitcast.142, f32[]{:T(128)} %broadcast.336), dimensions={1,2,4}, to_apply=%bitcast.142.reduce_sub_computation | reduce | bytes 8388612
  749.2 109.1 %reshape.375 = f32[32,1,32768]{2,1,0:T(1,128)} reshape(f32[65536,2,8]{2,1,0:T(2,128)} %reduce.2) | data formatting | bytes 8388608
  858.3 99.1 %all_to_all.15 = f32[32,1,32768]{2,1,0:T(1,128)} all-to-all(f32[32,1,32768]{2,1,0:T(1,128)} %reshape.375), channel_id=1, replica_groups=mesh['sub'=8,'sta'=4] {'sub','sta'}, dimensions={0} | all-to-all | bytes 8388608 | tf_op jit(solution)/shard_map/all_to_all | solution.py:113
  957.5 13.8 %reduce.3 = f32[32,32768]{1,0:T(8,128)} reduce(f32[32,1,32768]{2,1,0:T(1,128)} %all_to_all.15, f32[]{:T(128)} %broadcast.336), dimensions={1}, to_apply=%all_to_all.11.reduce_sub_computation | reduce | bytes 8388612 | tf_op jit(solution)/shard_map/all_to_all | solution.py:113
  971.2 171.1 %reshape.376 = f32[65536,1,1,2,1,8]{5,4,3,2,1,0:T(1,128)} reshape(f32[32,32768]{1,0:T(8,128)} %reduce.3) | data formatting | bytes 8388608
  1142.3 53.6 %copy.118 = f32[1,1,2,8,1,32,2048]{6,5,3,2,4,1,0:T(8,128)} copy(f32[1,1,2,8,1,32,2048]{3,2,6,5,4,1,0:T(2,128)} %bitcast.32) | data formatting | bytes 8388608 | tf_op jit(solution)/shard_map/all_to_all | solution.py:113
  1195.9 4.6 copy.107
  1201.3 6.4 copy.109
  1207.7 0.9 div.88
  (54 shorter events, 9.9 us)
Async XLA Ops:
  7.2 245.1 %copy-start = (bf16[1,2,32,64]{3,2,1,0:T(8,128)(2,1)S(1)}, bf16[1,2,32,64]{3,2,1,0:T(8,128)(2,1)}, u32[]{:S(2)}) copy-start(bf16[1,2,32,64]{3,2,1,0:T(8,128)(2,1)} %param.5) | copy-start | bytes 24580
  7.2 245.1 %all-gather.2.cloned.1.call-start = ((), (), s32[]{:S(2)}) async-start(), calls=%async_computation.1 | async-start | bytes 20971520 | tf_op jit(solution)/shard_map/all_gather | solution.py:80
  92.1 1.4 copy-start.5
  283.2 4.6 copy-start.3
  283.2 4.6 copy-start.4
  354.4 10.5 copy-start.2
  1201.3 7.3 copy-start.1
Sparse Core Ops, SparseCore 0:
  92.2 160.0 all-gather.1
where the time goes:
time: 1230 us; the launch traced here: 1220 us
  local copies, waits for them, and re-layouts  552 us (45%)
  other arithmetic  271 us (22%)
  waiting for transfers between devices  159 us (13%)
  matrix products  121 us (10%)
  blocking collectives  99.1 us (8%)
  between operations  14.6 us (1%)
    unnamed x18, local copies, waits for them, and re-layouts  294 us
    unnamed x2, other arithmetic  241 us
    all_gather x1, waiting for transfers between devices, shards(): shard_piece = lax.all_gather(shifted, 'sta', axis=2, tiled=True)  159 us
    another operation x3, local copies, waits for them, and re-layouts, shards(): jnp.stack([out_real * scale, out_imag * scale], axis=1)  120 us
    all_to_all x1, blocking collectives, shards(): lax.all_to_all(series[None], ('sub', 'sta'), split_axis=5, concat_axis=0,...  99.1 us
    gather x48, local copies, waits for them, and re-layouts  62.1 us
    all_to_all x2, local copies, waits for them, and re-layouts, shards(): lax.all_to_all(series[None], ('sub', 'sta'), split_axis=5, concat_axis=0,...  58.2 us
  transfers between devices with their start and end apart: 1, of which 1 were waited for; matrix products, arithmetic and copies ran while one was open for 0% of the time, Pallas kernels for 0%

commit v1 on v0

--- a/solution.py
+++ b/solution.py
@@ -110,7 +110,15 @@
     )
     n_sub = lax.axis_size("sub")
     n_sta = lax.axis_size("sta")
-    moved = lax.all_to_all(series[None], ("sub", "sta"), split_axis=5, concat_axis=0, tiled=True)
+    moved = jnp.concatenate(
+        lax.all_to_all(
+            jnp.stack(jnp.split(series[None], lax.axis_size(("sub", "sta")), axis=5)),
+            ("sub", "sta"),
+            0,
+            0,
+        ),
+        axis=0,
+    )
     moved = moved.reshape(n_sub, n_sta, sub_dev, 2, local_beams, trials, -1)
     moved = moved.transpose(0, 2, 3, 1, 4, 5, 6).reshape(
         n_sub * sub_dev, 2, n_sta * local_beams, trials, -1

time: 1230 us -> 511 us (0.42)
  local copies, waits for them, and re-layouts: 552 us -> 102 us
  other arithmetic: 271 us -> 10.8 us
    unnamed x18 -> x51, local copies, waits for them, and re-layouts: 294 us -> 15.5 us
    unnamed x2 -> x1, other arithmetic: 241 us -> 0.01 us
    another operation x3, local copies, waits for them, and re-layouts: 120 us -> 5.12 us  [shards(): jnp.stack([out_real * scale, out_imag * scale], axis=1)]
    all_to_all x2 -> x0, local copies, waits for them, and re-layouts: 58.2 us -> none  [shards(): lax.all_to_all(series[None], ('sub', 'sta'), split_axis=5, concat_axis=0,...]
    all_to_all x1 -> x0, other arithmetic: 13.8 us -> none  [shards(): lax.all_to_all(series[None], ('sub', 'sta'), split_axis=5, concat_axis=0,...]
where the time goes in v1:
time: 511 us; the launch traced here: 506 us
  waiting for transfers between devices  159 us (31%)
  matrix products  121 us (24%)
  local copies, waits for them, and re-layouts  102 us (20%)
  blocking collectives  98.7 us (19%)
  between operations  14.9 us (3%)
  other arithmetic  10.8 us (2%)
    all_gather x1, waiting for transfers between devices, shards(): shard_piece = lax.all_gather(shifted, 'sta', axis=2, tiled=True)  159 us
    all_to_all x1, blocking collectives, shards(): lax.all_to_all(jnp.stack(jnp.split(series[None], lax.axis_size(('sub', 's...  98.7 us
    gather x48, local copies, waits for them, and re-layouts  62.9 us
    unnamed x51, local copies, waits for them, and re-layouts  15.5 us
    dot_general x2, matrix products, right_dft(): jnp.einsum('...kt,tm->...km', x_real, sin_table, precision=HIGHEST)  15.5 us
    dot_general x2, matrix products, right_dft(): jnp.einsum('...kt,tm->...km', x_imag, sin_table, precision=HIGHEST)  15.4 us
    dot_general x2, matrix products, right_dft(): jnp.einsum('...kt,tm->...km', x_real, cos_table, precision=HIGHEST)  14.9 us
    dot_general x2, matrix products, right_dft(): jnp.einsum('...kt,tm->...km', x_imag, cos_table, precision=HIGHEST)  14.8 us
  transfers between devices with their start and end apart: 1, of which 1 were waited for; matrix products, arithmetic and copies ran while one was open for 0% of the time, Pallas kernels for 0%

profile of v1, /device:TPU:0, one launch (start us, length us, event | category | flops | bytes accessed | tf_op | source)
XLA Modules:
  0.0 505.7 jit_solution(10406041938670500814)
XLA Ops:
  7.2 6.5 %copy.72 = bf16[1,2,16,65536]{3,1,0,2:T(2,128)(2,1)S(1)} copy(bf16[1,2,16,65536]{3,2,1,0:T(8,128)(2,1)} %param.4) | data formatting | bytes 8388608 | tf_op args[0]
  13.8 9.2 %maximum_bitcast_fusion = bf16[16,1,2,131072]{3,2,1,0:T(2,128)(2,1)} fusion(bf16[1,2,16,65536]{3,1,0,2:T(2,128)(2,1)S(1)} %copy.72), kind=kLoop, calls=%fused_computation.6 | loop fusion | flops 16777216 | bytes 12582912 | tf_op jit(solution)/shard_map/vmap()/transpose | solution.py:73
  23.0 62.9 %while.1 = (s32[]{:T(128)}, bf16[16,1,2,131072]{3,2,1,0:T(2,128)(2,1)}, s32[16,4]{0,1:T(4,128)S(1)}, bf16[16,1,2,65536]{3,2,1,0:T(2,128)(2,1)}, s32[]{:T(128)}) while((s32[]{:T(128)}, bf16[16,1,2,131072]{3,2,1,0:T(2,128)(2,1)}, s32[16,4]{0,1:T(4,128)S(1)}, bf16[16,1,2,65536]{3,2,1,0:T(2,128)(2,1)}, s32[]{:T(128)}) %tuple.25), condition=%wide.while_cond, body=%wide.while_body.sunk | while | flops 2 | bytes 525937 | solution.py:73
  23.1 0.6 fusion.194
  23.7 3.3 dynamic-slice_dynamic-update-slice_fusion.2
  27.0 0.6 fusion.194
  27.6 3.3 dynamic-slice_dynamic-update-slice_fusion.2
  30.9 0.6 fusion.194
  31.5 3.3 dynamic-slice_dynamic-update-slice_fusion.2
  34.9 0.6 fusion.194
  35.5 3.3 dynamic-slice_dynamic-update-slice_fusion.2
  38.8 0.6 fusion.194
  39.4 3.3 dynamic-slice_dynamic-update-slice_fusion.2
  42.7 0.6 fusion.194
  43.3 3.3 dynamic-slice_dynamic-update-slice_fusion.2
  46.7 0.6 fusion.194
  47.3 3.3 dynamic-slice_dynamic-update-slice_fusion.2
  50.6 0.6 fusion.194
  51.2 3.3 dynamic-slice_dynamic-update-slice_fusion.2
  54.5 0.6 fusion.194
  55.1 3.3 dynamic-slice_dynamic-update-slice_fusion.2
  58.5 0.6 fusion.194
  59.1 3.3 dynamic-slice_dynamic-update-slice_fusion.2
  62.4 0.6 fusion.194
  63.0 3.3 dynamic-slice_dynamic-update-slice_fusion.2
  66.9 3.3 dynamic-slice_dynamic-update-slice_fusion.2
  70.3 0.6 fusion.194
  70.9 3.3 dynamic-slice_dynamic-update-slice_fusion.2
  74.8 3.3 dynamic-slice_dynamic-update-slice_fusion.2
  78.7 3.3 dynamic-slice_dynamic-update-slice_fusion.2
  82.6 3.3 dynamic-slice_dynamic-update-slice_fusion.2
  85.9 6.4 %copy.135 = bf16[16,1,2,65536]{3,0,2,1:T(8,128)(2,1)} copy(bf16[16,1,2,65536]{3,2,1,0:T(2,128)(2,1)} %get-tuple-element.9) | data formatting | bytes 8388608 | tf_op jit(solution)/shard_map/vmap()/gather | solution.py:73
  92.4 1.0 fusion.95
  93.9 158.7 %all-gather.2.cloned.1.call-done = bf16[1,2,64,65536]{3,2,1,0:T(8,128)(2,1)} async-done(((bf16[1,2,16,65536]{3,2,1,0:T(8,128)(2,1)}), bf16[1,2,64,65536]{3,2,1,0:T(8,128)(2,1)}) %all-gather.2.cloned.1.call-update) | async-done | bytes 16777232 | tf_op jit(solution)/shard_map/all_gather | solution.py:80
  252.6 4.6 fusion.1
  257.1 6.1 %convolution_add_fusion = f32[65536,8]{0,1:T(8,128)} fusion(f32[65536,8]{0,1:T(8,128)S(1)} %fusion.1, bf16[1,2,64,65536]{3,2,1,0:T(8,128)(2,1)} %all-gather.2.cloned.1.call-done, bf16[1,2,32,64]{3,2,1,0:T(8,128)(2,1)S(1)} %copy-done, s32[]{:T(128)S(6)} %add.214, s32[]{:T(128)S(6)} %select_n.87), kind=kOutput, calls=%fused_computation.2 | convolution fusion | flops 67633152 | bytes 12584968 | tf_op jit(solution)/shard_map/sbk,skt->bst/dot_general | solution.py:61
  263.2 2.5 copy.76
  265.7 4.1 fusion.50
  269.8 4.6 fusion
  274.4 6.1 %convolution_subtract_fusion = f32[65536,8]{0,1:T(8,128)} fusion(f32[65536,8]{0,1:T(8,128)S(1)} %fusion, bf16[1,2,64,65536]{3,2,1,0:T(8,128)(2,1)} %all-gather.2.cloned.1.call-done, bf16[1,2,32,64]{3,2,1,0:T(8,128)(2,1)S(1)} %copy-done, s32[]{:T(128)S(6)} %add.214, s32[]{:T(128)S(6)} %select_n.87), kind=kOutput, calls=%fused_computation.3 | convolution fusion | flops 67633152 | bytes 12584968 | tf_op jit(solution)/shard_map/sbk,skt->bst/dot_general | solution.py:58
  280.5 3.1 copy.75
  283.6 4.6 fusion.52
  288.2 2.9 convolution_subtract_fusion.1
  291.1 2.9 convolution_add_fusion.1
  294.0 4.9 fusion.25
  298.9 4.6 fusion.27
  303.5 4.6 fusion.20
  308.1 5.1 %fusion.17 = f32[8,256,256]{2,1,0:T(8,128)S(1)} fusion(f32[8,256,256]{2,1,0:T(8,128)S(1)} %fusion.27, f32[8,256,256]{2,1,0:T(8,128)S(1)} %convolution_add_fusion.1, f32[8,256,256]{2,1,0:T(8,128)S(1)} %convolution_subtract_fusion.1, f32[256,256]{0,1:T(8,128)S(1)} %copy.80, f32[256,256]{0,1:T(8,128)S(1)} %copy.77), kind=kOutput, calls=%fused_computation.40 | convolution fusion | flops 1613627392 | bytes 8912896 | tf_op jit(solution)/shard_map/...kt,tm->...km/dot_general | solution.py:46
  313.2 10.3 %fusion.46 = f32[8,256,256]{2,1,0:T(8,128)S(1)} fusion(f32[8,256,256]{2,1,0:T(8,128)S(1)} %fusion.20, f32[8,256,256]{2,1,0:T(8,128)S(1)} %fusion.17, f32[256,256]{1,0:T(8,128)S(1)} %multiply_divide_fusion, f32[8]{0:T(128)S(1)} %multiply_bitcast_fusion.2), kind=kOutput, calls=%fused_computation.71 | convolution fusion | flops 1613627392 | bytes 6553632 | tf_op jit(solution)/shard_map/...kt,tm->...km/dot_general | solution.py:44
  323.5 10.1 %fusion.44 = f32[8,256,256]{2,1,0:T(8,128)S(1)} fusion(f32[8,256,256]{2,1,0:T(8,128)S(1)} %fusion.17, f32[8,256,256]{2,1,0:T(8,128)S(1)} %fusion.20, f32[256,256]{1,0:T(8,128)S(1)} %multiply_divide_fusion, f32[8]{0:T(128)S(1)} %multiply_bitcast_fusion.2), kind=kOutput, calls=%fused_computation.69 | convolution fusion | flops 1613627392 | bytes 6553632 | tf_op jit(solution)/shard_map/...kt,tm->...km/dot_general | solution.py:47
  333.7 10.4 %multiply_add_fusion.1 = f32[8,256,256]{2,1,0:T(8,128)S(1)} fusion(f32[8,256,256]{2,1,0:T(8,128)S(1)} %fusion.46, f32[8,256,256]{2,1,0:T(8,128)S(1)} %fusion.17, f32[8,256,256]{2,1,0:T(8,128)S(1)} %fusion.20, f32[256,256]{1,0:T(8,128)S(1)} %multiply_divide_fusion, f32[8]{0:T(128)S(1)} %multiply_bitcast_fusion.2), kind=kOutput, calls=%fused_computation.39 | convolution fusion | flops 1614675968 | bytes 8650784 | tf_op jit(solution)/shard_map/...kt,tm->...km/dot_general | solution.py:46
  344.0 10.6 %multiply_subtract_fusion.1 = f32[8,256,256]{2,1,0:T(8,128)S(1)} fusion(f32[8,256,256]{2,1,0:T(8,128)S(1)} %fusion.44, f32[8,256,256]{2,1,0:T(8,128)S(1)} %fusion.20, f32[8,256,256]{2,1,0:T(8,128)S(1)} %fusion.17, f32[256,256]{1,0:T(8,128)S(1)} %multiply_divide_fusion, f32[8]{0:T(128)S(1)} %multiply_bitcast_fusion.2), kind=kOutput, calls=%fused_computation.38 | convolution fusion | flops 1614675968 | bytes 8650784 | tf_op jit(solution)/shard_map/...kt,tm->...km/dot_general | solution.py:49
  354.6 4.7 fusion.24
  359.4 5.7 %fusion.23 = f32[8,256,256]{2,1,0:T(8,128)} fusion(f32[8,256,256]{2,1,0:T(8,128)S(1)} %multiply_subtract_fusion.1, f32[8,256,256]{2,1,0:T(8,128)S(1)} %multiply_add_fusion.1, f32[256,256]{1,0:T(8,128)S(1)} %get-tuple-element.22, f32[256,256]{1,0:T(8,128)S(1)} %get-tuple-element.23), kind=kOutput, calls=%fused_computation.45 | convolution fusion | flops 1613103104 | bytes 6815744 | tf_op jit(solution)/shard_map/tk,bsjku->sbjtu/dot_general | solution.py:102
  365.1 5.8 %multiply_bitcast_fusion = f32[1,8,1,256,256]{3,4,1,2,0:T(8,128)} fusion(f32[8,256,256]{2,1,0:T(8,128)S(1)} %fusion.24, f32[8,256,256]{2,1,0:T(8,128)S(1)} %multiply_subtract_fusion.1, f32[8,256,256]{2,1,0:T(8,128)S(1)} %multiply_add_fusion.1, f32[256,256]{1,0:T(8,128)S(1)} %get-tuple-element.22, f32[256,256]{1,0:T(8,128)S(1)} %get-tuple-element.23), kind=kOutput, calls=%fused_computation.34 | convolution fusion | flops 1614151680 | bytes 8912896 | tf_op jit(solution)/shard_map/tk,bsjku->sbjtu/dot_general | solution.py:105
  370.9 3.1 copy.90
  374.0 3.3 stack.109
  377.3 7.9 %multiply_bitcast_fusion.1 = f32[1,8,1,256,256]{3,4,1,2,0:T(8,128)} fusion(f32[8,256,256]{2,1,0:T(8,128)} %fusion.23, f32[8,256,256]{2,1,0:T(8,128)S(1)} %multiply_add_fusion.1, f32[8,256,256]{2,1,0:T(8,128)} %copy-done.2, f32[256,256]{1,0:T(8,128)S(1)} %get-tuple-element.22, f32[256,256]{1,0:T(8,128)S(1)} %get-tuple-element.23), kind=kOutput, calls=%fused_computation.35 | convolution fusion | flops 1614151680 | bytes 8912896 | tf_op jit(solution)/shard_map/tk,bsjku->sbjtu/dot_general | solution.py:102
  385.2 1.9 copy.87
  387.2 1.7 stack.108
  388.9 1.9 constant_dynamic-update-slice_fusion.1
  391.9 98.7 %all_to_all.5 = f32[32,1,1,2,8,1,2048]{6,4,3,5,2,1,0:T(8,128)S(1)} all-to-all(f32[32,1,1,2,8,1,2048]{6,4,3,5,2,1,0:T(8,128)S(1)} %fusion.63), channel_id=1, replica_groups=mesh['sub'=8,'sta'=4] {'sub','sta'}, dimensions={0} | all-to-all | bytes 8388608 | tf_op jit(solution)/shard_map/all_to_all | solution.py:114
  490.8 6.4 %copy.123 = f32[8,2,32,1,2048]{4,3,2,1,0:T(1,128)} copy(f32[8,2,32,1,2048]{4,2,1,0,3:T(8,128)S(1)} %bitcast.309) | data formatting | bytes 8388608
  497.7 0.9 div.88
  (83 shorter events, 5.6 us)
Async XLA Ops:
  7.2 245.4 %copy-start = (bf16[1,2,32,64]{3,2,1,0:T(8,128)(2,1)S(1)}, bf16[1,2,32,64]{3,2,1,0:T(8,128)(2,1)}, u32[]{:S(2)}) copy-start(bf16[1,2,32,64]{3,2,1,0:T(8,128)(2,1)} %param.5) | copy-start | bytes 24580
  7.2 245.4 %all-gather.2.cloned.1.call-start = ((), (), s32[]{:S(2)}) async-start(), calls=%async_computation.1 | async-start | bytes 20971520 | tf_op jit(solution)/shard_map/all_gather | solution.py:80
  13.7 9.2 %copy-start.6 = (s32[16]{0:T(128)S(1)}, s32[16]{0:T(128)}, u32[]{:S(2)}) copy-start(s32[16]{0:T(128)} %param.6) | copy-start | bytes 196
  92.4 1.4 copy-start.7
  283.6 4.6 copy-start.3
  283.6 4.6 copy-start.4
  354.6 10.5 %copy-start.2 = (f32[8,256,256]{2,1,0:T(8,128)}, f32[8,256,256]{2,1,0:T(8,128)S(1)}, u32[]{:S(2)}) copy-start(f32[8,256,256]{2,1,0:T(8,128)S(1)} %multiply_subtract_fusion.1) | copy-start | bytes 6291460
  388.9 2.2 copy-start.5
  490.8 7.7 %copy-start.1 = (bf16[1,2,32,64]{3,2,1,0:T(8,128)(2,1)S(1)}, bf16[1,2,32,64]{3,2,1,0:T(8,128)(2,1)}, u32[]{:S(2)}) copy-start(bf16[1,2,32,64]{3,2,1,0:T(8,128)(2,1)} %param.5) | copy-start | bytes 24580
Sparse Core Ops, SparseCore 0:
  92.5 160.0 all-gather.1
